TPU v7x, 256 devices: a 4x2x16 block of a 4x16x16 slice. The times are simulated.
256 devices in a mesh: grp: 2 (over y), row: 32 (over z, core), col: 4 (over x).
Axes of the slice: x: 4, y: 2, z: 16, core: 2. Of those that a mesh axis runs over, the one named last changes fastest.
The devices are a block of a 4x16x16 slice.
Arguments:
- pair: bfloat16 [768, 384, 128], P(('grp', 'row'), 'col'), parts along dimension 0, may hold values from -6 to 6
- token_count: int32 [2], P('grp'), parts along dimension 0, may hold values from 288 to 384
- tri_in: bfloat16 [2, 128, 512], replicated, may hold values from -0.5 to 0.5
- tri_gate: bfloat16 [2, 128, 128], replicated, may hold values from -0.5 to 0.5
- tri_out: bfloat16 [2, 128, 128], replicated, may hold values from -0.5 to 0.5
- trans_in: bfloat16 [128, 1024], replicated, may hold values from -0.5 to 0.5
- trans_out: bfloat16 [512, 128], replicated, may hold values from -0.25 to 0.25
Outputs:
- pair_out: bfloat16 [768, 384, 128], P(('grp', 'row'), 'col'), parts along dimension 0
There are 2 independent parts, one for each index of `grp`. A program takes and returns all parts, laid end to end along the dimension named above; an argument that names none is the same for every part. Nothing has to cross between parts.
Inputs may be any that keep to these rules, and one draw needn't show every extreme that they name: `token_count`: the number of real tokens of the complex; pair entries with either token index at or past it are padding.
All inputs are finite; a program needn't handle non-finite values.
Results may differ from a plain program's by a relative error of at most 0.015.
Values may be sent and summed in bfloat16 or wider, within the bound.
A program may use at most 64 MiB of HBM per device.

v0:
```python
import jax
import jax.numpy as jnp
from jax import lax
from jax.sharding import Mesh
from jax.sharding import PartitionSpec as P

ROW = ("row_0", "row_1")
GRP_ROW = ("grp", "row_0", "row_1")


def split_up(value, dim, size):
    lengths = value.shape
    blocks = value.reshape(*lengths[:dim], size, lengths[dim] // size, *lengths[dim + 1 :])
    return jnp.moveaxis(blocks, dim, 0)


def sum_at_owner(value, axis, dim):
    blocks = split_up(value, dim, lax.axis_size(axis))
    arrived = lax.all_to_all(blocks, axis, split_axis=0, concat_axis=0, tiled=True)
    return arrived.sum(axis=0)


def sent_to_all(value, axis):
    copies = jnp.broadcast_to(value, (lax.axis_size(axis), *value.shape))
    return lax.all_to_all(copies, axis, split_axis=0, concat_axis=0, tiled=True)


def laid_out(blocks, dim):
    lengths = list(blocks.shape[1:])
    lengths[dim] *= blocks.shape[0]
    return jnp.moveaxis(blocks, 0, dim).reshape(lengths)


def gather_directly(value, axis, dim):
    blocks = sent_to_all(value, axis)
    return laid_out(blocks, dim)


def exchange_in_order(blocks, axes, sequence):
    lengths = [lax.axis_size(a) for a in axes]
    blocks = blocks.reshape(*lengths, *blocks.shape[1:])
    for k in sequence:
        blocks = lax.all_to_all(blocks, axes[k], split_axis=k, concat_axis=k, tiled=True)
    return blocks.reshape(-1, *blocks.shape[len(axes) :])


def two_step_exchange(value, groups, sequence, split_dim, concat_dim):
    size = lax.axis_size(groups[0]) * lax.axis_size(groups[1])
    blocks = split_up(value, split_dim, size)
    return laid_out(exchange_in_order(blocks, groups, sequence), concat_dim)


def layer_norm(values, along):
    average = jnp.mean(values, axis=along, keepdims=True)
    centred = values - average
    spread = jnp.mean(centred * centred, axis=along, keepdims=True)
    return centred * lax.rsqrt(spread + 1e-05)


def contract_rows(left_side, right_side):
    return jnp.einsum("hik,hjk->hij", left_side, right_side, preferred_element_type=jnp.float32)


def contract_columns(left_side, right_side):
    return jnp.einsum("hki,hkj->hij", left_side, right_side, preferred_element_type=jnp.float32)


def body(pair, token_count, tri_in, tri_gate, tri_out, trans_in, trans_out):
    tile_rows, tile_cols, pair_width = pair.shape
    hidden = tri_out.shape[1]
    ffn_width = trans_out.shape[0]
    row_place = lax.axis_index(ROW)
    col_place = lax.axis_index("col")
    row_first = row_place * tile_rows
    col_first = col_place * tile_cols
    token_limit = token_count[0]
    row_keep = (row_first + jnp.arange(tile_rows, dtype=jnp.int32) < token_limit).astype(
        jnp.float32
    )
    col_keep = (col_first + jnp.arange(tile_cols, dtype=jnp.int32) < token_limit).astype(
        jnp.float32
    )
    keep_mask = row_keep[:, None] * col_keep[None, :]

    def project(stream, which_side):
        normed = layer_norm(stream.astype(jnp.float32), 2).astype(jnp.bfloat16)
        weight = tri_in[which_side].reshape(pair_width, 4, hidden)
        projected = jnp.einsum("ijc,cgh->ghij", normed, weight, preferred_element_type=jnp.float32)
        left_side = (keep_mask * jax.nn.sigmoid(projected[2]) * projected[0]).astype(jnp.bfloat16)
        right_side = (keep_mask * jax.nn.sigmoid(projected[3]) * projected[1]).astype(jnp.bfloat16)
        gate_value = jax.nn.sigmoid(
            jnp.dot(normed, tri_gate[which_side], preferred_element_type=jnp.float32)
        )
        return (left_side, right_side, gate_value)

    def finish(stream, mixed_sum, gate_value, which_side):
        normed = layer_norm(mixed_sum, 0).astype(jnp.bfloat16)
        update = gate_value * jnp.einsum(
            "hij,hc->ijc", normed, tri_out[which_side], preferred_element_type=jnp.float32
        )
        return (stream.astype(jnp.float32) + keep_mask[:, :, None] * update).astype(jnp.bfloat16)

    left_side, right_side, gate_value = project(pair, 0)
    partial_rows = contract_rows(left_side, lax.all_gather(right_side, ROW, axis=1, tiled=True))
    mixed_sum = sum_at_owner(partial_rows, "col", 2)
    stream = finish(pair, mixed_sum, gate_value, 0)
    left_side, right_side, gate_value = project(stream, 1)
    left_rows = gather_directly(left_side, "col", 2)
    column_strip = two_step_exchange(left_rows, ("row_0", "row_1"), (1, 0), 2, 1)
    mixed_sum = contract_columns(column_strip, lax.all_gather(right_side, ROW, axis=1, tiled=True))
    stream = finish(stream, mixed_sum, gate_value, 1)
    normed = layer_norm(stream.astype(jnp.float32), 2).astype(jnp.bfloat16)
    inner_sum = jnp.dot(normed, trans_in, preferred_element_type=jnp.float32)
    activation = (jax.nn.silu(inner_sum[..., :ffn_width]) * inner_sum[..., ffn_width:]).astype(
        jnp.bfloat16
    )
    update = jnp.dot(activation, trans_out, preferred_element_type=jnp.float32)
    return (stream.astype(jnp.float32) + keep_mask[:, :, None] * update).astype(jnp.bfloat16)


def solution(mesh):
    torus = Mesh(
        mesh.devices.reshape(mesh.shape["grp"], 16, 2, mesh.shape["col"]),
        ("grp", "row_0", "row_1", "col"),
    )
    placed = (P(GRP_ROW, "col", None), P("grp"), P(), P(), P(), P(), P())
    return jax.shard_map(
        body, mesh=torus, in_specs=placed, out_specs=P(GRP_ROW, "col", None), check_vma=False
    )
```

profile of v0, /device:TPU:33, one launch (start us, length us, event | category | flops | bytes accessed | tf_op | source)
XLA Modules:
  0.0 327.6 jit_solution(5073324090975161739)
XLA Ops:
  7.2 1.1 convert_reduce_fusion
  8.4 1.4 fusion.20
  9.9 1.0 fusion.74
  11.1 1.5 convolution_bitcast_fusion.1
  12.6 1.1 fusion.37
  13.7 1.2 copy.55
  14.9 91.9 %all-gather.3.cloned.1.call-done = bf16[128,384,96]{0,2,1:T(8,128)(2,1)} async-done(((bf16[128,12,96]{0,2,1:T(8,128)(2,1)}), bf16[128,384,96]{0,2,1:T(8,128)(2,1)}) %all-gather.3.cloned.1.call-update) | async-done | bytes 9437200 | tf_op jit(solution)/shard_map/all_gather | solution.py:104
  106.8 15.6 %copy.56 = bf16[128,384,96]{2,1,0:T(8,128)(2,1)} copy(bf16[128,384,96]{0,2,1:T(8,128)(2,1)} %all-gather.3.cloned.1.call-done) | data formatting | bytes 18874368 | tf_op jit(solution)/shard_map/all_gather | solution.py:104
  122.4 9.2 %fusion.78 = f32[128,12,384]{2,1,0:T(8,128)S(1)} fusion(bf16[128,12,96]{2,1,0:T(8,128)(2,1)} %copy.55, bf16[128,384,96]{2,1,0:T(8,128)(2,1)} %copy.56), kind=kOutput, calls=%fused_computation.114 | convolution fusion | flops 113246208 | bytes 12091392 | tf_op jit(solution)/shard_map/hik,hjk->hij/dot_general | solution.py:61
  131.6 2.1 copy.57
  133.7 3.3 copy.58
  136.9 4.1 %all-to-all-start = ((f32[4,128,12,96]{1,3,2,0:T(8,128)}), f32[4,128,12,96]{1,3,2,0:T(8,128)S(1)}, u32[]{:S(2)}, u32[]{:S(2)}) async-start(f32[4,128,12,96]{1,3,2,0:T(8,128)} %copy.58), calls=%async_computation | async-start | bytes 4718592 | tf_op jit(solution)/shard_map/all_to_all | solution.py:19
  141.1 0.8 copy.81
  141.8 1.3 fusion.11
  143.1 26.6 %all-to-all-done = f32[4,128,12,96]{1,3,2,0:T(8,128)S(1)} async-done(((f32[4,128,12,96]{1,3,2,0:T(8,128)}), f32[4,128,12,96]{1,3,2,0:T(8,128)S(1)}, u32[]{:S(2)}, u32[]{:S(2)}) %all-to-all-start) | async-done | bytes 2359328 | tf_op jit(solution)/shard_map/all_to_all | solution.py:19
  172.4 1.1 fusion.23
  173.7 17.4 %all_to_all.20 = bf16[4,128,12,96]{1,3,2,0:T(8,128)(2,1)S(1)} all-to-all(bf16[4,128,12,96]{1,3,2,0:T(8,128)(2,1)S(1)} %broadcast_in_dim.2), channel_id=1, replica_groups=mesh['grp'=2,'row_0'=16,'row_1'=2,'col'=4] {'col'}, dimensions={0} | all-to-all | bytes 2359296 | tf_op jit(solution)/shard_map/all_to_all | solution.py:25
  191.0 1.1 copy.62
  192.1 2.2 reshape_reshape.3
  194.8 7.1 %all_to_all.21 = bf16[16,2,128,12,12]{2,0,4,3,1:T(8,128)(2,1)S(1)} all-to-all(bf16[16,2,128,12,12]{2,0,4,3,1:T(8,128)(2,1)S(1)} %copy.63), channel_id=1, replica_groups=mesh['grp'=2,'row_0'=16,'row_1'=2,'col'=4] {'row_1'}, dimensions={1} | all-to-all | bytes 2359296 | tf_op jit(solution)/shard_map/all_to_all | solution.py:43
  201.9 2.2 copy.64
  204.1 6.6 %all-to-all-start.3 = ((bf16[16,2,128,12,12]{2,1,4,3,0:T(2,128)(2,1)}), bf16[16,2,128,12,12]{2,1,4,3,0:T(2,128)(2,1)S(1)}, u32[]{:S(2)}, u32[]{:S(2)}) async-start(bf16[16,2,128,12,12]{2,1,4,3,0:T(2,128)(2,1)} %copy.64), calls=%async_computation.3 | async-start | bytes 2359296 | tf_op jit(solution)/shard_map/all_to_all | solution.py:43
  211.2 66.2 %all-to-all-done.3 = bf16[16,2,128,12,12]{2,1,4,3,0:T(2,128)(2,1)S(1)} async-done(((bf16[16,2,128,12,12]{2,1,4,3,0:T(2,128)(2,1)}), bf16[16,2,128,12,12]{2,1,4,3,0:T(2,128)(2,1)S(1)}, u32[]{:S(2)}, u32[]{:S(2)}) %all-to-all-start.3) | async-done | bytes 1179680 | tf_op jit(solution)/shard_map/all_to_all | solution.py:43
  277.4 1.0 copy.65
  278.5 0.8 copy.66
  279.3 1.2 reshape.165
  280.4 2.2 copy.67
  282.6 12.4 %all-gather.5.cloned.1.call-done = bf16[128,384,96]{0,2,1:T(8,128)(2,1)} async-done(((bf16[128,12,96]{0,2,1:T(8,128)(2,1)}), bf16[128,384,96]{0,2,1:T(8,128)(2,1)}) %all-gather.5.cloned.1.call-update) | async-done | bytes 9437200 | tf_op jit(solution)/shard_map/all_gather | solution.py:110
  295.0 15.6 %copy.68 = bf16[128,384,96]{2,1,0:T(8,128)(2,1)} copy(bf16[128,384,96]{0,2,1:T(8,128)(2,1)} %all-gather.5.cloned.1.call-done) | data formatting | bytes 18874368 | tf_op jit(solution)/shard_map/all_gather | solution.py:110
  310.6 5.8 %fusion.76 = (f32[12,96]{1,0:T(8,128)S(1)}, f32[128,12,96]{2,1,0:T(8,128)S(1)}) fusion(bf16[128,384,12]{1,2,0:T(8,128)(2,1)S(1)} %copy.67, bf16[128,384,96]{2,1,0:T(8,128)(2,1)} %copy.68), kind=kOutput, calls=%fused_computation.112 | convolution fusion | flops 113392512 | bytes 11211264 | tf_op jit(solution)/shard_map/hki,hkj->hij/dot_general | solution.py:65
  318.4 0.8 fusion.53
  319.3 1.5 fusion.16
  (46 shorter events, 6.0 us)
Async XLA Ops:
  6.5 311.8 %copy-start = (bf16[128,1024]{1,0:T(8,128)(2,1)S(1)}, bf16[128,1024]{1,0:T(8,128)(2,1)}, u32[]{:S(2)}) copy-start(bf16[128,1024]{1,0:T(8,128)(2,1)} %param.12) | copy-start | bytes 786436
  6.6 100.3 %all-gather.3.cloned.1.call-start = ((), (), s32[]{:S(2)}) async-start(), calls=%async_computation.4 | async-start | bytes 9732096 | tf_op jit(solution)/shard_map/all_gather | solution.py:104
  9.9 1.2 copy-start.5
  136.9 4.9 %copy-start.1 = (bf16[12,96,128]{2,1,0:T(8,128)(2,1)S(1)}, bf16[12,96,128]{2,1,0:T(8,128)(2,1)}, u32[]{:S(2)}) copy-start(bf16[12,96,128]{2,1,0:T(8,128)(2,1)} %param.7) | copy-start | bytes 884740
  136.9 32.8 %all-to-all-start = ((f32[4,128,12,96]{1,3,2,0:T(8,128)}), f32[4,128,12,96]{1,3,2,0:T(8,128)S(1)}, u32[]{:S(2)}, u32[]{:S(2)}) async-start(f32[4,128,12,96]{1,3,2,0:T(8,128)} %copy.58), calls=%async_computation | async-start | bytes 4718592 | tf_op jit(solution)/shard_map/all_to_all | solution.py:19
  141.1 153.9 %all-gather.5.cloned.1.call-start = ((), (), s32[]{:S(2)}) async-start(), calls=%async_computation.5 | async-start | bytes 9732096 | tf_op jit(solution)/shard_map/all_gather | solution.py:110
  169.7 0.8 copy-start.3
  170.0 1.8 copy-start.2
  201.9 8.8 %copy-start.7 = (bf16[2,128,128]{2,1,0:T(8,128)(2,1)S(1)}, bf16[2,128,128]{2,1,0:T(8,128)(2,1)}, u32[]{:S(2)}) copy-start(bf16[2,128,128]{2,1,0:T(8,128)(2,1)} %param.10) | copy-start | bytes 196612
  204.1 73.3 %all-to-all-start.3 = ((bf16[16,2,128,12,12]{2,1,4,3,0:T(2,128)(2,1)}), bf16[16,2,128,12,12]{2,1,4,3,0:T(2,128)(2,1)S(1)}, u32[]{:S(2)}, u32[]{:S(2)}) async-start(bf16[16,2,128,12,12]{2,1,4,3,0:T(2,128)(2,1)} %copy.64), calls=%async_computation.3 | async-start | bytes 2359296 | tf_op jit(solution)/shard_map/all_to_all | solution.py:43
  316.4 0.8 copy-start.4
  318.4 0.9 copy-start.6
Sparse Core Ops, SparseCore 0:
  13.8 92.9 all-gather.2
  173.6 121.3 all-gather.4
where the time goes:
time: 329 us; the launch traced here: 328 us
  waiting for transfers between devices  197 us (60%)
  local copies, waits for them, and re-layouts  51.5 us (16%)
  blocking collectives  24.4 us (7%)
  matrix products  22.5 us (7%)
  between operations  14.4 us (4%)
  starting transfers between devices  10.7 us (3%)
  other arithmetic  6.82 us (2%)
    all_gather x2, waiting for transfers between devices, body(): lax.all_gather(right_side, ROW, axis=1, tiled=True)  104 us
    all_to_all x1, waiting for transfers between devices, exchange_in_order(): lax.all_to_all(blocks, axes[k], split_axis=k, concat_axis=k, tiled=True)  66.2 us
    all_gather x2, local copies, waits for them, and re-layouts, body(): lax.all_gather(right_side, ROW, axis=1, tiled=True)  31.1 us
    all_to_all x1, waiting for transfers between devices, sum_at_owner(): lax.all_to_all(blocks, axis, split_axis=0, concat_axis=0, tiled=True)  26.6 us
    all_to_all x1, blocking collectives, sent_to_all(): return lax.all_to_all(copies, axis, split_axis=0, concat_axis=0, tiled=True)  17.4 us
    dot_general x1, matrix products, contract_rows(): jnp.einsum('hik,hjk->hij', left_side, right_side, preferred_element_type=...  9.19 us
    all_to_all x1, blocking collectives, exchange_in_order(): lax.all_to_all(blocks, axes[k], split_axis=k, concat_axis=k, tiled=True)  7.07 us
    all_to_all x1, starting transfers between devices, exchange_in_order(): lax.all_to_all(blocks, axes[k], split_axis=k, concat_axis=k, tiled=True)  6.6 us
  transfers between devices with their start and end apart: 4, of which 4 were waited for; matrix products, arithmetic and copies ran while one was open for 5% of the time, Pallas kernels for 0%

commit v1 on v0

--- a/solution.py
+++ b/solution.py
@@ -101,7 +101,12 @@
         return (stream.astype(jnp.float32) + keep_mask[:, :, None] * update).astype(jnp.bfloat16)
 
     left_side, right_side, gate_value = project(pair, 0)
-    partial_rows = contract_rows(left_side, lax.all_gather(right_side, ROW, axis=1, tiled=True))
+    partial_rows = contract_rows(
+        left_side,
+        jnp.concatenate(
+            lax.all_to_all(jnp.stack([right_side] * lax.axis_size(ROW)), ROW, 0, 0), axis=1
+        ),
+    )
     mixed_sum = sum_at_owner(partial_rows, "col", 2)
     stream = finish(pair, mixed_sum, gate_value, 0)
     left_side, right_side, gate_value = project(stream, 1)

time: 329 us -> 673 us (2.05)
  waiting for transfers between devices: 197 us -> 508 us
  starting transfers between devices: 10.7 us -> 43.8 us
    all_to_all x0 -> x1, waiting for transfers between devices: none -> 402 us  [body(): lax.all_to_all(jnp.stack([right_side] * lax.axis_size(ROW)), ROW, 0, 0)]
    all_gather x2 -> x1, waiting for transfers between devices: 104 us -> 14 us  [body(): lax.all_gather(right_side, ROW, axis=1, tiled=True)]
    all_to_all x0 -> x1, starting transfers between devices: none -> 25.5 us  [body(): lax.all_to_all(jnp.stack([right_side] * lax.axis_size(ROW)), ROW, 0, 0)]
    all_gather x2 -> x1, local copies, waits for them, and re-layouts: 31.1 us -> 15.6 us  [body(): lax.all_gather(right_side, ROW, axis=1, tiled=True)]
    reshape x0 -> x1, local copies, waits for them, and re-layouts: none -> 14 us  [body(): jnp.concatenate(lax.all_to_all(jnp.stack([right_side] * lax.axis_size(ROW...]
    all_to_all x1, starting transfers between devices: 6.6 us -> 13.8 us  [exchange_in_order(): lax.all_to_all(blocks, axes[k], split_axis=k, concat_axis=k, tiled=True)]
  transfers between devices with their start and end apart: 4 -> 4, of which waited for: 4 -> 4; matrix products, arithmetic and copies ran while one was open for 5% -> 2% of each run, Pallas kernels for 0% -> 0%
where the time goes in v1:
time: 673 us; the launch traced here: 672 us
  waiting for transfers between devices  508 us (75%)
  local copies, waits for them, and re-layouts  55.7 us (8%)
  starting transfers between devices  43.8 us (7%)
  blocking collectives  24.3 us (4%)
  matrix products  19 us (3%)
  between operations  14.4 us (2%)
    all_to_all x1, waiting for transfers between devices, body(): lax.all_to_all(jnp.stack([right_side] * lax.axis_size(ROW)), ROW, 0, 0)  402 us
    all_to_all x1, waiting for transfers between devices, exchange_in_order(): lax.all_to_all(blocks, axes[k], split_axis=k, concat_axis=k, tiled=True)  66.2 us
    all_to_all x1, waiting for transfers between devices, sum_at_owner(): lax.all_to_all(blocks, axis, split_axis=0, concat_axis=0, tiled=True)  26.4 us
    all_to_all x1, starting transfers between devices, body(): lax.all_to_all(jnp.stack([right_side] * lax.axis_size(ROW)), ROW, 0, 0)  25.5 us
    all_to_all x1, blocking collectives, sent_to_all(): return lax.all_to_all(copies, axis, split_axis=0, concat_axis=0, tiled=True)  17.4 us
    all_gather x1, local copies, waits for them, and re-layouts, body(): lax.all_gather(right_side, ROW, axis=1, tiled=True)  15.6 us
    reshape x1, local copies, waits for them, and re-layouts, body(): jnp.concatenate(lax.all_to_all(jnp.stack([right_side] * lax.axis_size(ROW...  14 us
    all_gather x1, waiting for transfers between devices, body(): lax.all_gather(right_side, ROW, axis=1, tiled=True)  14 us
  transfers between devices with their start and end apart: 4, of which 4 were waited for; matrix products, arithmetic and copies ran while one was open for 2% of the time, Pallas kernels for 0%

profile of v1, /device:TPU:33, one launch (start us, length us, event | category | flops | bytes accessed | tf_op | source)
XLA Modules:
  0.0 671.9 jit_solution(17294297833036400189)
XLA Ops:
  7.2 1.1 convert_reduce_fusion
  8.4 1.4 fusion.20
  9.9 1.0 fusion.68
  11.1 1.5 convolution_bitcast_fusion.1
  12.8 5.8 stack.5
  18.6 25.5 %all-to-all-start = ((bf16[32,128,12,96]{1,3,2,0:T(8,128)(2,1)}), bf16[32,128,12,96]{1,3,2,0:T(8,128)(2,1)}, u32[]{:S(2)}, u32[]{:S(2)}) async-start(bf16[32,128,12,96]{1,3,2,0:T(8,128)(2,1)} %stack.5), calls=%async_computation | async-start | bytes 18874368 | tf_op jit(solution)/shard_map/all_to_all | solution.py:107
  44.3 1.2 copy.71
  45.5 401.8 %all-to-all-done = bf16[32,128,12,96]{1,3,2,0:T(8,128)(2,1)} async-done(((bf16[32,128,12,96]{1,3,2,0:T(8,128)(2,1)}), bf16[32,128,12,96]{1,3,2,0:T(8,128)(2,1)}, u32[]{:S(2)}, u32[]{:S(2)}) %all-to-all-start) | async-done | bytes 9437216 | tf_op jit(solution)/shard_map/all_to_all | solution.py:107
  447.3 14.0 %copy.72 = bf16[128,384,96]{1,2,0:T(8,128)(2,1)} copy(bf16[128,384,96]{0,2,1:T(8,128)(2,1)} %bitcast.14) | data formatting | bytes 18874368 | tf_op jit(solution)/shard_map/reshape | solution.py:106
  461.4 5.6 fusion.72
  467.0 2.1 copy.73
  469.1 3.3 copy.74
  472.3 4.5 all-to-all-start.1
  477.6 1.3 fusion.11
  478.9 26.4 %all-to-all-done.1 = f32[4,128,12,96]{1,3,2,0:T(8,128)S(1)} async-done(((f32[4,128,12,96]{1,3,2,0:T(8,128)}), f32[4,128,12,96]{1,3,2,0:T(8,128)S(1)}, u32[]{:S(2)}, u32[]{:S(2)}) %all-to-all-start.1) | async-done | bytes 2359328 | tf_op jit(solution)/shard_map/all_to_all | solution.py:19
  507.9 1.1 fusion.44
  509.2 17.4 %all_to_all.25 = bf16[4,128,12,96]{1,3,2,0:T(8,128)(2,1)S(1)} all-to-all(bf16[4,128,12,96]{1,3,2,0:T(8,128)(2,1)S(1)} %broadcast_in_dim.2), channel_id=1, replica_groups=mesh['grp'=2,'row_0'=16,'row_1'=2,'col'=4] {'col'}, dimensions={0} | all-to-all | bytes 2359296 | tf_op jit(solution)/shard_map/all_to_all | solution.py:25
  526.6 1.1 copy.80
  527.7 2.2 reshape_reshape.3
  530.4 6.9 %all_to_all.26 = bf16[16,2,128,12,12]{2,0,4,3,1:T(8,128)(2,1)S(1)} all-to-all(bf16[16,2,128,12,12]{2,0,4,3,1:T(8,128)(2,1)S(1)} %copy.81), channel_id=1, replica_groups=mesh['grp'=2,'row_0'=16,'row_1'=2,'col'=4] {'row_1'}, dimensions={1} | all-to-all | bytes 2359296 | tf_op jit(solution)/shard_map/all_to_all | solution.py:43
  537.3 2.2 copy.82
  539.5 13.8 %all-to-all-start.4 = ((bf16[16,2,128,12,12]{2,1,4,3,0:T(2,128)(2,1)}), bf16[16,2,128,12,12]{2,1,4,3,0:T(2,128)(2,1)S(1)}, u32[]{:S(2)}, u32[]{:S(2)}) async-start(bf16[16,2,128,12,12]{2,1,4,3,0:T(2,128)(2,1)} %copy.82), calls=%async_computation.4 | async-start | bytes 2359296 | tf_op jit(solution)/shard_map/all_to_all | solution.py:43
  553.9 66.2 %all-to-all-done.4 = bf16[16,2,128,12,12]{2,1,4,3,0:T(2,128)(2,1)S(1)} async-done(((bf16[16,2,128,12,12]{2,1,4,3,0:T(2,128)(2,1)}), bf16[16,2,128,12,12]{2,1,4,3,0:T(2,128)(2,1)S(1)}, u32[]{:S(2)}, u32[]{:S(2)}) %all-to-all-start.4) | async-done | bytes 1179680 | tf_op jit(solution)/shard_map/all_to_all | solution.py:43
  620.1 1.0 copy.83
  621.1 0.8 copy.84
  621.9 1.2 reshape.168
  623.1 2.2 copy.87
  625.3 14.0 %all-gather.2.cloned.1.call-done = bf16[128,384,96]{0,2,1:T(8,128)(2,1)} async-done(((bf16[128,12,96]{0,2,1:T(8,128)(2,1)}), bf16[128,384,96]{0,2,1:T(8,128)(2,1)}) %all-gather.2.cloned.1.call-update) | async-done | bytes 9437200 | tf_op jit(solution)/shard_map/all_gather | solution.py:115
  639.3 15.6 %copy.88 = bf16[128,384,96]{2,1,0:T(8,128)(2,1)} copy(bf16[128,384,96]{0,2,1:T(8,128)(2,1)} %all-gather.2.cloned.1.call-done) | data formatting | bytes 18874368 | tf_op jit(solution)/shard_map/all_gather | solution.py:115
  654.8 5.8 fusion.70
  662.7 0.8 fusion.46
  663.6 1.5 fusion.16
  (47 shorter events, 7.2 us)
Async XLA Ops:
  6.5 656.1 %copy-start = (bf16[128,1024]{1,0:T(8,128)(2,1)S(1)}, bf16[128,1024]{1,0:T(8,128)(2,1)}, u32[]{:S(2)}) copy-start(bf16[128,1024]{1,0:T(8,128)(2,1)} %param.12) | copy-start | bytes 786436
  9.9 3.0 copy-start.5
  18.6 428.7 %all-to-all-start = ((bf16[32,128,12,96]{1,3,2,0:T(8,128)(2,1)}), bf16[32,128,12,96]{1,3,2,0:T(8,128)(2,1)}, u32[]{:S(2)}, u32[]{:S(2)}) async-start(bf16[32,128,12,96]{1,3,2,0:T(8,128)(2,1)} %stack.5), calls=%async_computation | async-start | bytes 18874368 | tf_op jit(solution)/shard_map/all_to_all | solution.py:107
  472.3 5.2 copy-start.1
  472.3 33.0 %all-to-all-start.1 = ((f32[4,128,12,96]{1,3,2,0:T(8,128)}), f32[4,128,12,96]{1,3,2,0:T(8,128)S(1)}, u32[]{:S(2)}, u32[]{:S(2)}) async-start(f32[4,128,12,96]{1,3,2,0:T(8,128)} %copy.74), calls=%async_computation.1 | async-start | bytes 4718592 | tf_op jit(solution)/shard_map/all_to_all | solution.py:19
  476.8 162.5 %all-gather.2.cloned.1.call-start = ((), (), s32[]{:S(2)}) async-start(), calls=%async_computation.5 | async-start | bytes 9732096 | tf_op jit(solution)/shard_map/all_gather | solution.py:115
  505.3 0.8 copy-start.3
  505.6 1.8 copy-start.2
  537.3 16.1 %copy-start.7 = (bf16[2,128,128]{2,1,0:T(8,128)(2,1)S(1)}, bf16[2,128,128]{2,1,0:T(8,128)(2,1)}, u32[]{:S(2)}) copy-start(bf16[2,128,128]{2,1,0:T(8,128)(2,1)} %param.10) | copy-start | bytes 196612
  539.5 80.5 %all-to-all-start.4 = ((bf16[16,2,128,12,12]{2,1,4,3,0:T(2,128)(2,1)}), bf16[16,2,128,12,12]{2,1,4,3,0:T(2,128)(2,1)S(1)}, u32[]{:S(2)}, u32[]{:S(2)}) async-start(bf16[16,2,128,12,12]{2,1,4,3,0:T(2,128)(2,1)} %copy.82), calls=%async_computation.4 | async-start | bytes 2359296 | tf_op jit(solution)/shard_map/all_to_all | solution.py:43
  660.7 0.8 copy-start.4
  662.7 0.9 copy-start.6
Sparse Core Ops, SparseCore 0:
  509.2 130.0 all-gather.1
